TPU v7x, 32 devices: a whole 2x2x4 slice. The times are simulated.
32 devices in a mesh: groups: 2 (over y), ctx: 8 (over z, x), head: 2 (over core).
Axes of the slice: x: 2, y: 2, z: 4, core: 2. Of those that a mesh axis runs over, the one named last changes fastest.
Arguments:
- keys_values: bfloat16 [2, 8192, 1024], P(None, ('groups', 'ctx'), 'head'), parts along dimension 1, may hold values from -6 to 6
- span_order: int32 [32], P('groups'), parts along dimension 0, may hold values from 0 to 15, as said below
- page_table: int32 [64], P('groups'), parts along dimension 0, may hold values from 0 to 31, as said below
Outputs:
- paged_cache: bfloat16 [2, 64, 128, 1024], P(None, ('groups', 'ctx', 'head')), parts along dimension 1
There are 2 independent parts, one for each index of `groups`. A program takes and returns all parts, laid end to end along the dimension named above; each array names one. Nothing has to cross between parts.
Inputs may be any that keep to these rules, and one draw needn't show every extreme that they name: `span_order`: blocks 2 c and 2 c + 1 hold two spans whose numbers add to 15; every span is held once. A permutation of the slots in which page p goes to a slot of p // 2, that is page_table[p] // 2 == p // 2.
All inputs are finite; a program needn't handle non-finite values.
Results may differ from a plain program's by a relative error of at most 0.001.
Values may be sent and summed in bfloat16 or wider, within the bound.
A program may use at most 64 MiB of HBM per device.

v0:
```python
import functools

import jax
import jax.numpy as jnp
from jax import lax
from jax.experimental import pallas as pl
from jax.experimental.pallas import tpu as pltpu
from jax.sharding import PartitionSpec as P

PAGE = 128
UNIT = 8
LANES = 128
COL_CHUNKS = 1
INNER_EVERY = 0
MESH = pl.DeviceIdType.MESH


class Chunk:
    def __init__(self, kv, unit, units, col, width, full_width, takers):
        self.kv, self.unit, self.units, self.col, self.width = kv, unit, units, col, width
        self.takers = takers
        self.row_blocks = min(takers, units)
        self.share_units = units // self.row_blocks
        self.col_blocks = takers // self.row_blocks
        self.share_width = width // self.col_blocks
        self.parts = 1 if self.share_width == full_width else 2


def plan(n2, width):
    page_units = PAGE // UNIT
    units = min(page_units, n2)
    col_chunks = max(1, min(COL_CHUNKS, width // (n2 // units * LANES)))
    chunk_width = width // col_chunks
    chunks = []
    for kv in range(2):
        for unit in range(0, page_units, units):
            for col in range(0, width, chunk_width):
                inner = INNER_EVERY and len(chunks) % INNER_EVERY == 0
                takers = n2 // 2 if inner else n2
                chunks.append(Chunk(kv, unit, units, col, chunk_width, width, takers))
    return chunks


def grid(n2):
    grid_rows = n2 // 2
    reach = max(1, grid_rows // 4)
    return grid_rows, reach, -(-(grid_rows - 1) // reach) + 1


def kernel(n2, pages, width, x_ref, order_ref, table_ref, out_ref, *scratch):
    chunks = plan(n2, width)
    count = len(chunks)
    stored = scratch[0:count]
    halves = scratch[count : 2 * count]
    shares = scratch[2 * count : 3 * count]
    routed = scratch[3 * count : 4 * count]
    holder, source_page, load_sem, send1, recv1, send2, recv2, hops = scratch[4 * count :]

    group = lax.axis_index("groups")
    ctx = lax.axis_index("ctx")
    head = lax.axis_index("head")
    me = ctx * 2 + head
    my_half = me // n2
    my_place = lax.rem(me, n2)

    def device(j):
        return (group, j // 2, lax.rem(j, 2))

    def load(k):
        c = chunks[k]
        return pltpu.make_async_copy(
            x_ref.at[c.kv, :, :, pl.ds(c.unit, c.units), :, pl.ds(c.col, c.width)],
            stored[k],
            load_sem.at[k],
        )

    for k in range(count):
        load(k).start()

    barrier = pltpu.get_barrier_semaphore()

    grid_rows, reach, stages = grid(n2)
    row, col = ctx // 2, lax.rem(ctx, 2)
    other = ctx + 1 - 2 * col
    neighbours = 3 + 2 * (jnp.minimum(row, reach) + jnp.minimum(grid_rows - 1 - row, reach))

    def greet(stage):
        sem = barrier if stage == 1 else hops.at[stage]

        def signal(to_ctx, to_head):
            pl.semaphore_signal(
                sem, inc=1, device_id=(group, to_ctx, to_head), device_id_type=MESH
            )

        for step in range(1, reach + 1):
            for sign in (-1, 1):
                to_row = row + sign * step

                @pl.when(jnp.logical_and(to_row >= 0, to_row < grid_rows))
                def _(step=sign * step):
                    for h in range(2):
                        signal(ctx + 2 * step, h)

        signal(ctx, 1 - head)
        for h in range(2):
            signal(other, h)

    def greeted(stage):
        pl.semaphore_wait(barrier if stage == 1 else hops.at[stage], neighbours)

    greet(1)

    first_is_upper = (order_ref[2 * ctx] >= n2).astype(jnp.int32)
    for k in range(count):
        load(k).wait()
        for half in range(2):
            block = first_is_upper if half == 0 else 1 - first_is_upper
            c = chunks[k]
            for share in range(c.takers):
                unit = share // c.col_blocks * c.share_units
                col = share % c.col_blocks * c.share_width
                for page in range(pages):
                    halves[k][half, share, page] = stored[k][
                        block, page, unit : unit + c.share_units, :, col : col + c.share_width
                    ]

    def base(k, half):
        return (n2 - chunks[k].takers) * (1 - half)

    def taking(k):
        share = my_place - base(k, my_half)
        return jnp.logical_and(share >= 0, share < chunks[k].takers)

    def spread(k, half, share):
        return halves[k].at[half, share], shares[k].at[ctx, head]

    def sends(k, d):
        takers = chunks[k].takers
        half = lax.rem(my_half + 1 + d // takers, 2)
        share = lax.rem(me + d, takers)
        return half, share, half * n2 + base(k, half) + share

    def send(k, to_ctx, to_head):
        j = to_ctx * 2 + to_head
        half = j // n2
        share = lax.rem(j, n2) - base(k, half)

        def start():
            src, dst = spread(k, half, share)
            pltpu.make_async_remote_copy(
                src_ref=src,
                dst_ref=dst,
                send_sem=send1.at[k, j],
                recv_sem=recv1.at[k],
                device_id=(group, to_ctx, to_head),
                device_id_type=MESH,
            ).start()

        if chunks[k].takers == n2:
            start()
        else:
            pl.when(jnp.logical_and(share >= 0, share < chunks[k].takers))(start)

    def send_stage(k, stage):
        for step in range(1 - grid_rows, grid_rows):
            for cross in range(2):
                if max(1, -(-abs(step) // reach) + cross) != stage:
                    continue
                to_ctx = (other if cross else ctx) + 2 * step
                if step == 0 and not cross:
                    send(k, ctx, 1 - head)

                    @pl.when(taking(k))
                    def _():
                        src, dst = spread(k, my_half, my_place - base(k, my_half))
                        pltpu.make_async_copy(src, dst, recv1.at[k]).start()

                else:

                    @pl.when(jnp.logical_and(row + step >= 0, row + step < grid_rows))
                    def _(to_ctx=to_ctx):
                        for h in range(2):
                            send(k, to_ctx, h)

    early = [2, 2, 1]
    for stage in range(1, stages + 1):
        greeted(stage)
        if stage < stages:
            greet(stage + 1)
        for k in range(early[min(stage, len(early)) - 1]):
            send_stage(k, stage)

    for k in range(count):
        for stage in range(stages, 0, -1):
            if k >= early[min(stage, len(early)) - 1]:
                send_stage(k, stage)

    @pl.loop(0, n2)
    def _(i):
        span = my_half * n2 + i

        def find(b, at):
            return jnp.where(order_ref[b] == span, b // 2, at)

        holder[i] = lax.fori_loop(0, 2 * n2, find, jnp.int32(0))
        for slot in range(pages):
            page = jnp.int32(0)
            for p in range(pages):
                page = jnp.where(table_ref[span * pages + p] == span * pages + slot, p, page)
            source_page[i * pages + slot] = page

    def deliver(k, i, h):
        c = chunks[k]
        share = my_place - base(k, my_half)
        at = lax.rem(share, c.col_blocks) * c.share_width + h * width + c.col
        dst = out_ref.at[
            c.kv,
            :,
            pl.ds(c.unit + share // c.col_blocks * c.share_units, c.share_units),
            :,
            pl.ds(pl.multiple_of(at, LANES), 2 // c.parts * c.share_width),
        ]
        return routed[k].at[i, h], dst

    for k in range(count):

        @pl.when(taking(k))
        def _(k=k):
            pltpu.make_async_copy(shares[k], shares[k], recv1.at[k]).wait()

            @pl.loop(0, n2)
            def _(d):
                i = lax.rem(my_place + d, n2)
                c = holder[i]
                for slot in range(pages):
                    page = source_page[i * pages + slot]
                    for h in range(2):
                        if chunks[k].parts == 2:
                            routed[k][i, h, slot] = shares[k][c, h, page]
                        else:
                            routed[k][i, 0, slot, :, :, h * width : (h + 1) * width] = shares[k][
                                c, h, page
                            ]

            @pl.loop(0, n2)
            def _(d):
                i = lax.rem(my_place + d, n2)
                j = my_half * n2 + i
                for h in range(chunks[k].parts):
                    src, dst = deliver(k, i, h)

                    @pl.when(j != me)
                    def _():
                        pltpu.make_async_remote_copy(
                            src_ref=src,
                            dst_ref=dst,
                            send_sem=send2.at[k, i, h],
                            recv_sem=recv2.at[k],
                            device_id=device(j),
                            device_id_type=MESH,
                        ).start()

                    @pl.when(j == me)
                    def _():
                        pltpu.make_async_copy(src, dst, recv2.at[k]).start()

    for k in range(count):
        c = chunks[k]

        @pl.loop(0, 2 * c.takers)
        def _(d, k=k):
            half, share, j = sends(k, d)

            @pl.when(j != me)
            def _():
                src, _ = spread(k, half, share)
                pltpu.make_async_copy(src, src, send1.at[k, j]).wait()

        @pl.when(taking(k))
        def _(k=k):
            @pl.loop(1, n2)
            def _(d):
                i = lax.rem(my_place + d, n2)
                for h in range(chunks[k].parts):
                    src = routed[k].at[i, h]
                    pltpu.make_async_copy(src, src, send2.at[k, i, h]).wait()

    for k in range(count):
        both = halves[k]
        pltpu.make_async_copy(both, both, recv2.at[k]).wait()


def per_device(keys_values, span_order, page_table):
    _, tok_rows, width = keys_values.shape
    n_ctx = lax.axis_size("ctx")
    n2 = n_ctx * lax.axis_size("head") // 2
    pages = tok_rows // 2 // PAGE
    chunks = plan(n2, width)
    count = len(chunks)
    dtype = keys_values.dtype
    x = keys_values.reshape(2, 2, pages, PAGE // UNIT, UNIT, width)
    out = pl.pallas_call(
        functools.partial(kernel, n2, pages, width),
        out_shape=jax.ShapeDtypeStruct((2, pages, PAGE // UNIT, UNIT, 2 * width), dtype),
        in_specs=[
            pl.BlockSpec(memory_space=pl.ANY),
            pl.BlockSpec(memory_space=pltpu.SMEM),
            pl.BlockSpec(memory_space=pltpu.SMEM),
        ],
        out_specs=pl.BlockSpec(memory_space=pl.ANY),
        scratch_shapes=[pltpu.VMEM((2, pages, c.units, UNIT, c.width), dtype) for c in chunks]
        + [
            pltpu.VMEM((2, c.takers, pages, c.share_units, UNIT, c.share_width), dtype)
            for c in chunks
        ]
        + [
            pltpu.VMEM((n_ctx, 2, pages, c.share_units, UNIT, c.share_width), dtype)
            for c in chunks
        ]
        + [
            pltpu.VMEM(
                (n2, c.parts, pages, c.share_units, UNIT, 2 // c.parts * c.share_width), dtype
            )
            for c in chunks
        ]
        + [
            pltpu.SMEM((n2,), jnp.int32),
            pltpu.SMEM((n2 * pages,), jnp.int32),
            pltpu.SemaphoreType.DMA((count,)),
            pltpu.SemaphoreType.DMA((count, 2 * n2)),
            pltpu.SemaphoreType.DMA((count,)),
            pltpu.SemaphoreType.DMA((count, n2, 2)),
            pltpu.SemaphoreType.DMA((count,)),
            pltpu.SemaphoreType.REGULAR((grid(n2)[2] + 1,)),
        ],
        compiler_params=pltpu.CompilerParams(collective_id=0, has_side_effects=True),
    )(x, span_order, page_table)
    return out.reshape(2, pages, PAGE, 2 * width)


def solution(mesh):
    in_specs = (P(None, ("groups", "ctx"), "head"), P("groups"), P("groups"))
    out_specs = P(None, ("groups", "ctx", "head"), None, None)
    return jax.shard_map(
        per_device, mesh=mesh, in_specs=in_specs, out_specs=out_specs, check_vma=False
    )
```

profile of v0, /device:TPU:1, one launch (start us, length us, event | category | flops | bytes accessed | tf_op | source)
XLA Modules:
  0.0 38.5 jit_solution(4686700638341324822)
XLA Ops:
  0.0 36.3 %shard_map.37 = bf16[2,2,16,8,1024]{4,3,2,1,0:T(8,128)(2,1)} custom-call(bf16[2,2,2,16,8,512]{5,4,3,2,1,0:T(8,128)(2,1)} %bitcast.3, s32[16]{0:T(128)} %order_ref.1, s32[32]{0:T(128)} %table_ref.1), custom_call_target="tpu_custom_call" | custom-call | tf_op jit(solution)/shard_map/pallas_call | solution.py:302
  36.3 2.3 %copy.5 = bf16[2,2,128,1024]{3,2,1,0:T(8,128)(2,1)} copy(bf16[2,2,128,1024]{3,2,1,0:T(8,128)(2,1)} %bitcast.2) | data formatting | bytes 2097152
where the time goes:
time: 38.7 us; the launch traced here: 38.5 us
  Pallas kernels  36.3 us (94%)
  local copies, waits for them, and re-layouts  2.26 us (6%)
    pallas_call x1, Pallas kernels, per_device(): pl.pallas_call(functools.partial(kernel, n2, pages, width), out_shape=jax...  36.3 us
    unnamed x1, local copies, waits for them, and re-layouts  2.26 us

commit v1 on v0

--- a/solution.py
+++ b/solution.py
@@ -301,9 +301,9 @@
     x = keys_values.reshape(2, 2, pages, PAGE // UNIT, UNIT, width)
     out = pl.pallas_call(
         functools.partial(kernel, n2, pages, width),
-        out_shape=jax.ShapeDtypeStruct((2, pages, PAGE // UNIT, UNIT, 2 * width), dtype),
+        out_shape=pltpu.VMEM((2, pages, PAGE // UNIT, UNIT, 2 * width), dtype),
         in_specs=[
-            pl.BlockSpec(memory_space=pl.ANY),
+            pl.BlockSpec(memory_space=pltpu.HBM),
             pl.BlockSpec(memory_space=pltpu.SMEM),
             pl.BlockSpec(memory_space=pltpu.SMEM),
         ],

time: 38.7 us -> 37.3 us (0.964)
  local copies, waits for them, and re-layouts: 2.26 us -> 0.97 us
    unnamed x1, local copies, waits for them, and re-layouts: 2.26 us -> 0.97 us
where the time goes in v1:
time: 37.3 us; the launch traced here: 37.1 us
  Pallas kernels  36.2 us (97%)
  local copies, waits for them, and re-layouts  0.97 us (3%)
    pallas_call x1, Pallas kernels, per_device(): pl.pallas_call(functools.partial(kernel, n2, pages, width), out_shape=plt...  36.2 us
    unnamed x1, local copies, waits for them, and re-layouts  0.97 us

profile of v1, /device:TPU:1, one launch (start us, length us, event | category | flops | bytes accessed | tf_op | source)
XLA Modules:
  0.0 37.1 jit_solution(18197966579737142566)
XLA Ops:
  0.0 36.2 %shard_map.37 = bf16[2,2,16,8,1024]{4,3,2,1,0:T(8,128)(2,1)S(1)} custom-call(bf16[2,2,2,16,8,512]{5,4,3,2,1,0:T(8,128)(2,1)} %bitcast.3, s32[16]{0:T(128)} %order_ref.1, s32[32]{0:T(128)} %table_ref.1), custom_call_target="tpu_custom_call" | custom-call | tf_op jit(solution)/shard_map/pallas_call | solution.py:302
  36.2 1.0 %copy.5 = bf16[2,2,128,1024]{3,2,1,0:T(8,128)(2,1)} copy(bf16[2,2,128,1024]{3,2,1,0:T(8,128)(2,1)S(1)} %bitcast.2) | data formatting | bytes 2097152

commit v2 on v1

v2 whole, which is shorter than its diff:
```python
import functools

import jax
import jax.numpy as jnp
from jax import lax
from jax.experimental import pallas as pl
from jax.experimental.pallas import tpu as pltpu
from jax.sharding import PartitionSpec as P

PAGE = 128
UNIT = 8
LANES = 128
REACH = 4
HEAD = [2, 2]
EARLY = (3, 3)
AHEAD = (0, 1)
LEAD = 2
FAR_FIRST = 1
MESH = pl.DeviceIdType.MESH


class Chunk:
    def __init__(self, kv, unit, units, width, takers):
        self.kv, self.unit, self.units, self.width = kv, unit, units, width
        self.takers = takers
        self.row_blocks = min(takers, units)
        self.share_units = units // self.row_blocks
        self.col_blocks = takers // self.row_blocks
        self.share_width = width // self.col_blocks
        self.parts = 1 if self.share_width == width else 2
        self.taker_rows = takers // 4

    def first_row(self, rows, half):
        return rows // 2 - self.taker_rows * (1 - half)


def plan(n2, width):
    page_units = PAGE // UNIT
    inner = min(page_units, n2 // 2)
    sizes = [inner] * (2 * page_units // inner)
    if inner >= 4 * (n2 // 2 * LANES // width):
        head = [p * inner // 4 for p in HEAD]
        sizes = head + sizes[sum(HEAD) // 4 :]
    chunks, at = [], 0
    for units in sizes:
        chunks.append(Chunk(at // page_units, at % page_units, units, width, n2 // 2))
        at += units
    return chunks


def order(count, takes):
    early, ahead = min(EARLY[takes], count), AHEAD[takes]
    steps = []
    for k in range(early):
        steps += [("X", k), ("A", k)]
    steps += [("X", k) for k in range(early, count)] + [("G", 0)]
    steps += [("B", k) for k in range(early)]
    ready = early
    for k in range(count + LEAD):
        if k < count:
            steps.append(("F", k))
            while ready < min(count, k + 1 + ahead):
                steps.append(("S", ready))
                ready += 1
        if takes and 0 <= k - LEAD < count:
            steps.append(("T", k - LEAD))
    return steps


def grid(n2):
    rows = n2 // 2
    reach = max(1, rows // REACH)
    away = rows // 2 + n2 // 8 - 1
    return rows, reach, max(-(-away // reach), -(-(rows // 2 - 1) // reach) + 1)


def kernel(n2, pages, width, x_ref, order_in, table_in, out_ref, *scratch):
    chunks = plan(n2, width)
    count = len(chunks)
    stored = scratch[0:count]
    halves = scratch[count : 2 * count]
    relays = scratch[2 * count : 3 * count]
    shares = scratch[3 * count : 4 * count]
    routed = scratch[4 * count : 5 * count]
    (order_ref, table_ref, holder, source_page, table_sem, load_sem) = scratch[5 * count : 5 * count + 6]
    (send1, recv1, send_relay, recv_relay, send2, recv2, hops) = scratch[5 * count + 6 :]

    group = lax.axis_index("groups")
    ctx = lax.axis_index("ctx")
    head = lax.axis_index("head")
    me = ctx * 2 + head
    my_half = me // n2
    rows, reach, stages = grid(n2)
    row, col = ctx // 2, lax.rem(ctx, 2)
    other = ctx + 1 - 2 * col

    def share_of(c):
        return me - c.first_row(rows, my_half) * 4

    def taking(c):
        return jnp.logical_and(share_of(c) >= 0, share_of(c) < c.takers)

    def load(k):
        c = chunks[k]
        return pltpu.make_async_copy(
            x_ref.at[c.kv, :, :, pl.ds(c.unit, c.units)], stored[k], load_sem.at[k]
        )

    def fetch(n):
        src, dst = ((order_in, order_ref), (table_in, table_ref))[n]
        return pltpu.make_async_copy(src, dst, table_sem.at[n])

    fetch(0).start()
    load(0).start()

    barrier = pltpu.get_barrier_semaphore()
    neighbours = 3 + 2 * (jnp.minimum(row, reach) + jnp.minimum(rows - 1 - row, reach))

    def greet(stage):
        sem = barrier if stage == 1 else hops.at[stage]

        def signal(to_ctx, to_head):
            pl.semaphore_signal(
                sem, inc=1, device_id=(group, to_ctx, to_head), device_id_type=MESH
            )

        for step in range(1, reach + 1):
            for sign in (-1, 1):
                to_row = row + sign * step

                @pl.when(jnp.logical_and(to_row >= 0, to_row < rows))
                def _(step=sign * step):
                    for h in range(2):
                        signal(ctx + 2 * step, h)

        signal(ctx, 1 - head)
        for h in range(2):
            signal(other, h)

    def greeted(stage):
        pl.semaphore_wait(barrier if stage == 1 else hops.at[stage], neighbours)

    greet(1)
    fetch(1).start()
    for k in range(1, count):
        load(k).start()
    fetch(0).wait()

    both_halves = (1 - my_half, my_half) if FAR_FIRST else (my_half, 1 - my_half)

    first_is_upper = (order_ref[2 * ctx] >= n2).astype(jnp.int32)

    def split(k):
        c = chunks[k]
        load(k).wait()
        for half in range(2):
            block = first_is_upper if half == 0 else 1 - first_is_upper
            for share in range(c.takers):
                unit = share // c.col_blocks * c.share_units
                at = share % c.col_blocks * c.share_width
                for page in range(pages):
                    halves[k][half * c.takers + share, page] = stored[k][
                        block, page, unit : unit + c.share_units, :, at : at + c.share_width
                    ]

    def send(k, half, share, to_ctx, to_head, dst, recv_sem):
        pltpu.make_async_remote_copy(
            src_ref=halves[k].at[half * chunks[k].takers + share],
            dst_ref=dst,
            send_sem=send1.at[k],
            recv_sem=recv_sem,
            device_id=(group, to_ctx, to_head),
            device_id_type=MESH,
        ).start()

    def cross(k):
        c = chunks[k]
        for half in both_halves:
            for t in range(c.taker_rows):
                same = row == c.first_row(rows, half) + t

                def out(dst, recv_sem, half=half, t=t):
                    for h in range(2):
                        share = t * 4 + (1 - col) * 2 + h
                        send(k, half, share, other, h, dst, recv_sem)

                @pl.when(same)
                def _(out=out):
                    out(shares[k].at[ctx, head], recv1.at[k])

                @pl.when(jnp.logical_not(same))
                def _(out=out, half=half, t=t):
                    out(relays[k].at[half * chunks[k].taker_rows + t, head], recv_relay.at[k, half])

    def straight(k, stage=None):
        c = chunks[k]
        for half in both_halves:
            for t in range(c.taker_rows):
                to_row = c.first_row(rows, half) + t
                away = jnp.abs(to_row - row)
                dst = shares[k].at[ctx, head]

                if stage is None or stage == 1:

                    @pl.when(away == 0)
                    def _(half=half, t=t, dst=dst):
                        send(k, half, t * 4 + col * 2 + 1 - head, ctx, 1 - head, dst, recv1.at[k])
                        own = halves[k].at[half * c.takers + t * 4 + col * 2 + head]
                        pltpu.make_async_copy(own, dst, recv1.at[k]).start()

                far = away > 0
                if stage is not None:
                    far = jnp.logical_and(
                        away > (stage - 1) * reach, away <= stage * reach
                    )

                @pl.when(far)
                def _(half=half, t=t, dst=dst, to_row=to_row):
                    for h in range(2):
                        send(k, half, t * 4 + col * 2 + h, to_row * 2 + col, h, dst, recv1.at[k])

    def forward(k):
        c = chunks[k]
        for half in both_halves:
            first = c.first_row(rows, half)
            top = half * c.taker_rows
            inside = jnp.logical_and(row >= first, row < first + c.taker_rows)

            def arrived(n, half=half, top=top):
                part = relays[k].at[pl.ds(top, n)]
                pltpu.make_async_copy(part, part, recv_relay.at[k, half]).wait()

            @pl.when(jnp.logical_not(inside))
            def _(arrived=arrived):
                arrived(c.taker_rows)

            if c.taker_rows > 1:

                @pl.when(inside)
                def _(arrived=arrived):
                    arrived(c.taker_rows - 1)

            for t in range(c.taker_rows):
                to_row = first + t

                @pl.when(row != to_row)
                def _(at=top + t, to_row=to_row):
                    pltpu.make_async_remote_copy(
                        src_ref=relays[k].at[at],
                        dst_ref=shares[k].at[other],
                        send_sem=send_relay.at[k],
                        recv_sem=recv1.at[k],
                        device_id=(group, to_row * 2 + col, head),
                        device_id_type=MESH,
                    ).start()

    def tables():
        fetch(1).wait()

        @pl.loop(0, n2)
        def _(i):
            span = my_half * n2 + i

            def find(b, at):
                return jnp.where(order_ref[b] == span, b // 2, at)

            holder[i] = lax.fori_loop(0, 2 * n2, find, jnp.int32(0), unroll=16)
            for slot in range(pages):
                page = jnp.int32(0)
                for p in range(pages):
                    page = jnp.where(table_ref[span * pages + p] == span * pages + slot, p, page)
                source_page[i * pages + slot] = page

    def deliver(k, i, h):
        c = chunks[k]
        my_share = share_of(c)
        at = lax.rem(my_share, c.col_blocks) * c.share_width + h * width
        dst = out_ref.at[
            c.kv,
            :,
            pl.ds(c.unit + my_share // c.col_blocks * c.share_units, c.share_units),
            :,
            pl.ds(pl.multiple_of(at, LANES), 2 // c.parts * c.share_width),
        ]
        return routed[k].at[i, h], dst

    def take(k):
        @pl.when(taking(chunks[k]))
        def _():
            pltpu.make_async_copy(shares[k], shares[k], recv1.at[k]).wait()
            start = my_half * (n2 // 2)

            @pl.loop(0, n2)
            def _(d):
                i = lax.rem(start + d, n2)
                c = holder[i]
                for slot in range(pages):
                    page = source_page[i * pages + slot]
                    for h in range(2):
                        if chunks[k].parts == 2:
                            routed[k][i, h, slot] = shares[k][c, h, page]
                        else:
                            routed[k][i, 0, slot, :, :, h * width : (h + 1) * width] = shares[k][
                                c, h, page
                            ]

            @pl.loop(0, n2)
            def _(d):
                i = lax.rem(start + d, n2)
                j = my_half * n2 + i
                for h in range(chunks[k].parts):
                    src, dst = deliver(k, i, h)

                    @pl.when(j != me)
                    def _():
                        pltpu.make_async_remote_copy(
                            src_ref=src,
                            dst_ref=dst,
                            send_sem=send2.at[k],
                            recv_sem=recv2.at[k],
                            device_id=(group, j // 2, lax.rem(j, 2)),
                            device_id_type=MESH,
                        ).start()

                    @pl.when(j == me)
                    def _():
                        pltpu.make_async_copy(src, dst, recv2.at[k]).start()

    for k in range(count):
        split(k)
    greeted(1)
    if stages > 1:
        greet(2)

    def later(k):
        for stage in range(2, stages + 1):
            straight(k, stage)

    def climb(k):
        for stage in range(2, stages + 1):
            greeted(stage)
            if stage < stages:
                greet(stage + 1)

    steps = {
        "X": cross,
        "A": lambda k: straight(k, 1),
        "B": later,
        "S": straight,
        "F": forward,
        "T": take,
        "G": climb,
    }
    inner_row = taking(chunks[0])
    tables()

    def follow(steps_in_order):
        for name, k in steps_in_order:
            steps[name](k)

    @pl.when(inner_row)
    def _():
        follow(order(count, 1))

    @pl.when(jnp.logical_not(inner_row))
    def _():
        follow(order(count, 0))

    for k in range(count):

        def sent(buf, n, sem):
            part = buf.at[pl.ds(0, n)]
            pltpu.make_async_copy(part, part, sem).wait()

        c = chunks[k]

        @pl.when(taking(c))
        def _(k=k, c=c, sent=sent):
            sent(halves[k], 2 * c.takers - 1, send1.at[k])
            sent(relays[k], 2 * c.taker_rows - 1, send_relay.at[k])
            sent(routed[k], n2 - 1, send2.at[k])

        @pl.when(jnp.logical_not(taking(c)))
        def _(k=k, c=c, sent=sent):
            sent(halves[k], 2 * c.takers, send1.at[k])
            sent(relays[k], 2 * c.taker_rows, send_relay.at[k])

    for k in range(count):
        pltpu.make_async_copy(halves[k], halves[k], recv2.at[k]).wait()


def per_device(keys_values, span_order, page_table):
    _, tok_rows, width = keys_values.shape
    n_ctx = lax.axis_size("ctx")
    n2 = n_ctx * lax.axis_size("head") // 2
    pages = tok_rows // 2 // PAGE
    chunks = plan(n2, width)
    count = len(chunks)
    stages = grid(n2)[2]
    dtype = keys_values.dtype
    x = keys_values.reshape(2, 2, pages, PAGE // UNIT, UNIT, width)

    def share(c, *lead):
        return pltpu.VMEM((*lead, pages, c.share_units, UNIT, c.share_width), dtype)

    out = pl.pallas_call(
        functools.partial(kernel, n2, pages, width),
        out_shape=pltpu.VMEM((2, pages, PAGE // UNIT, UNIT, 2 * width), dtype),
        in_specs=[
            pl.BlockSpec(memory_space=pltpu.HBM),
            pl.BlockSpec(memory_space=pltpu.HBM),
            pl.BlockSpec(memory_space=pltpu.HBM),
        ],
        out_specs=pl.BlockSpec(memory_space=pl.ANY),
        scratch_shapes=[pltpu.VMEM((2, pages, c.units, UNIT, width), dtype) for c in chunks]
        + [share(c, 2 * c.takers) for c in chunks]
        + [share(c, 2 * c.taker_rows, 2) for c in chunks]
        + [share(c, n_ctx, 2) for c in chunks]
        + [
            pltpu.VMEM(
                (n2, c.parts, pages, c.share_units, UNIT, 2 // c.parts * c.share_width), dtype
            )
            for c in chunks
        ]
        + [
            pltpu.SMEM(span_order.shape, jnp.int32),
            pltpu.SMEM(page_table.shape, jnp.int32),
            pltpu.SMEM((n2,), jnp.int32),
            pltpu.SMEM((n2 * pages,), jnp.int32),
            pltpu.SemaphoreType.DMA((2,)),
            pltpu.SemaphoreType.DMA((count,)),
            pltpu.SemaphoreType.DMA((count,)),
            pltpu.SemaphoreType.DMA((count,)),
            pltpu.SemaphoreType.DMA((count,)),
            pltpu.SemaphoreType.DMA((count, 2)),
            pltpu.SemaphoreType.DMA((count,)),
            pltpu.SemaphoreType.DMA((count,)),
            pltpu.SemaphoreType.REGULAR((stages + 1,)),
        ],
        compiler_params=pltpu.CompilerParams(collective_id=0, has_side_effects=True),
    )(x, span_order, page_table)
    return out.reshape(2, pages, PAGE, 2 * width)


def solution(mesh):
    in_specs = (P(None, ("groups", "ctx"), "head"), P("groups"), P("groups"))
    out_specs = P(None, ("groups", "ctx", "head"), None, None)
    return jax.shard_map(
        per_device, mesh=mesh, in_specs=in_specs, out_specs=out_specs, check_vma=False
    )
```

time: 37.3 us -> 35.5 us (0.952)
  Pallas kernels: 36.2 us -> 34.4 us
    pallas_call x1, Pallas kernels: 36.2 us -> 34.4 us  [per_device(): pl.pallas_call(functools.partial(kernel, n2, pages, width), out_shape=plt...]
where the time goes in v2:
time: 35.5 us; the launch traced here: 35.4 us
  Pallas kernels  34.4 us (97%)
  local copies, waits for them, and re-layouts  0.97 us (3%)
    pallas_call x1, Pallas kernels, per_device(): pl.pallas_call(functools.partial(kernel, n2, pages, width), out_shape=plt...  34.4 us
    unnamed x1, local copies, waits for them, and re-layouts  0.97 us

profile of v2, /device:TPU:1, one launch (start us, length us, event | category | flops | bytes accessed | tf_op | source)
XLA Modules:
  0.0 35.4 jit_solution(3891024876018181334)
XLA Ops:
  0.0 34.4 %shard_map.37 = bf16[2,2,16,8,1024]{4,3,2,1,0:T(8,128)(2,1)S(1)} custom-call(bf16[2,2,2,16,8,512]{5,4,3,2,1,0:T(8,128)(2,1)} %bitcast.3, s32[16]{0:T(128)} %order_in.1, s32[32]{0:T(128)} %table_in.1), custom_call_target="tpu_custom_call" | custom-call | tf_op jit(solution)/shard_map/pallas_call | solution.py:406
  34.4 1.0 %copy.5 = bf16[2,2,128,1024]{3,2,1,0:T(8,128)(2,1)} copy(bf16[2,2,128,1024]{3,2,1,0:T(8,128)(2,1)S(1)} %bitcast.2) | data formatting | bytes 2097152

commit v3 on v2

--- a/solution.py
+++ b/solution.py
@@ -328,6 +328,7 @@
 
     for k in range(count):
         split(k)
+    tables()
     greeted(1)
     if stages > 1:
         greet(2)
@@ -352,7 +353,6 @@
         "G": climb,
     }
     inner_row = taking(chunks[0])
-    tables()
 
     def follow(steps_in_order):
         for name, k in steps_in_order:

time: 35.5 us -> 35.7 us (level)
  no operation moved by 1% of the time
where the time goes in v3:
time: 35.7 us; the launch traced here: 35.5 us
  Pallas kernels  34.6 us (97%)
  local copies, waits for them, and re-layouts  0.97 us (3%)
    pallas_call x1, Pallas kernels, per_device(): pl.pallas_call(functools.partial(kernel, n2, pages, width), out_shape=plt...  34.6 us
    unnamed x1, local copies, waits for them, and re-layouts  0.97 us

profile of v3, /device:TPU:1, one launch (start us, length us, event | category | flops | bytes accessed | tf_op | source)
XLA Modules:
  0.0 35.5 jit_solution(10470605516003867379)
XLA Ops:
  0.0 34.6 %shard_map.37 = bf16[2,2,16,8,1024]{4,3,2,1,0:T(8,128)(2,1)S(1)} custom-call(bf16[2,2,2,16,8,512]{5,4,3,2,1,0:T(8,128)(2,1)} %bitcast.3, s32[16]{0:T(128)} %order_in.1, s32[32]{0:T(128)} %table_in.1), custom_call_target="tpu_custom_call" | custom-call | tf_op jit(solution)/shard_map/pallas_call | solution.py:406
  34.6 1.0 %copy.5 = bf16[2,2,128,1024]{3,2,1,0:T(8,128)(2,1)} copy(bf16[2,2,128,1024]{3,2,1,0:T(8,128)(2,1)S(1)} %bitcast.2) | data formatting | bytes 2097152
